TPU v7x, 32 devices: a whole 2x2x4 slice. The times are simulated.
32 devices in a mesh: ep: 4 (over y, x), fsdp: 8 (over z, core).
Axes of the slice: x: 2, y: 2, z: 4, core: 2. Of those that a mesh axis runs over, the one named last changes fastest.
Arguments:
- train_gate: float32 [128, 2048, 768], P('ep', 'fsdp'), may hold values from -0.1875 to 0.1875
- other_gate: bfloat16 [128, 2048, 768], P('ep', 'fsdp'), may hold values from -0.0625 to 0.0625
- train_up: float32 [128, 2048, 768], P('ep', 'fsdp'), may hold values from -0.1875 to 0.1875
- other_up: bfloat16 [128, 2048, 768], P('ep', 'fsdp'), may hold values from -0.0625 to 0.0625
- router_weight: float32 [2048, 128], P('fsdp', 'ep'), may hold values from -0.125 to 0.125
- router_gain: float32 [2048], P('fsdp'), may hold values from 0.25 to 1.75
Outputs:
- ready_gate: bfloat16 [128, 2048, 768], P(('ep', 'fsdp'))
- ready_up: bfloat16 [128, 2048, 768], P(('ep', 'fsdp'))
- scale_gate: float32 [128, 768], P(('ep', 'fsdp'))
- scale_up: float32 [128, 768], P(('ep', 'fsdp'))
- serve_router: bfloat16 [2048, 128], replicated
All inputs are finite; a program needn't handle non-finite values. Where the computation divides by a largest or mean magnitude, that divisor is 1e-20 or more.
Results may differ from a plain program's by a relative error of at most 0.013.
Values may be sent and summed in bfloat16 or wider, within the bound.
A program may use at most 192 MiB of HBM per device.

v0:
```python
import jax
import jax.numpy as jnp
from jax import lax
from jax.sharding import PartitionSpec as P

D_MODEL = 2048


def shards(train_gate, other_gate, train_up, other_up, router_weight, router_gain):
    latest_gate = train_gate + other_gate.astype(jnp.float32)
    latest_up = train_up + other_up.astype(jnp.float32)
    total_gate, total_up = (
        lax.psum(jnp.sum(jnp.abs(latest_gate), axis=1).astype(jnp.bfloat16), "fsdp").astype(
            jnp.float32
        ),
        lax.psum(jnp.sum(jnp.abs(latest_up), axis=1).astype(jnp.bfloat16), "fsdp").astype(
            jnp.float32
        ),
    )
    scale_gate = total_gate / D_MODEL
    scale_up = total_up / D_MODEL
    narrow_gate, narrow_up = (
        (latest_gate / jnp.expand_dims(scale_gate, 1)).astype(jnp.bfloat16),
        (latest_up / jnp.expand_dims(scale_up, 1)).astype(jnp.bfloat16),
    )
    ready_gate, ready_up = (
        lax.all_to_all(narrow_gate, "fsdp", split_axis=0, concat_axis=1, tiled=True),
        lax.all_to_all(narrow_up, "fsdp", split_axis=0, concat_axis=1, tiled=True),
    )
    scale_gate = lax.dynamic_slice_in_dim(
        scale_gate, lax.axis_index("fsdp") * ready_gate.shape[0], ready_gate.shape[0], axis=0
    )
    scale_up = lax.dynamic_slice_in_dim(
        scale_up, lax.axis_index("fsdp") * ready_up.shape[0], ready_up.shape[0], axis=0
    )
    part_router = (router_weight * router_gain[:, None]).astype(jnp.bfloat16)
    row_router = lax.all_gather(part_router, "fsdp", axis=0, tiled=True)
    serve_router = lax.all_gather(row_router, "ep", axis=1, tiled=True)
    return (ready_gate, ready_up, scale_gate, scale_up, serve_router)


def solution(mesh):
    placed = (
        P("ep", "fsdp", None),
        P("ep", "fsdp", None),
        P("ep", "fsdp", None),
        P("ep", "fsdp", None),
        P("fsdp", "ep"),
        P("fsdp"),
    )
    return jax.shard_map(
        shards,
        mesh=mesh,
        in_specs=placed,
        out_specs=(
            P(("ep", "fsdp"), None, None),
            P(("ep", "fsdp"), None, None),
            P(("ep", "fsdp"), None),
            P(("ep", "fsdp"), None),
            P(),
        ),
        check_vma=False,
    )
```

profile of v0, /device:TPU:0, one launch (start us, length us, event | category | flops | bytes accessed | tf_op | source)
XLA Modules:
  0.0 711.2 jit_solution(16841271009129784802)
XLA Ops:
  7.2 0.0 all-reduce.3.cloned.1.call-start
  7.2 25.2 %abs_reduce_fusion = (bf16[32,768]{1,0:T(8,128)(2,1)}, bf16[32,768]{1,0:T(8,128)(2,1)}) fusion(f32[32,256,768]{2,1,0:T(8,128)} %param.8, bf16[32,256,768]{2,1,0:T(8,128)(2,1)} %param.9, f32[32,256,768]{2,1,0:T(8,128)} %param.6, bf16[32,256,768]{2,1,0:T(8,128)(2,1)} %param.7), kind=kLoop, calls=%fused_computation.1 | loop fusion | flops 50282496 | bytes 75595776 | tf_op jit(solution)/shard_map/reduce_sum | solution.py:16
  32.4 0.0 all-reduce.3.cloned.1.call-update
  32.4 55.4 %all-reduce.3.cloned.1.call-done = (bf16[32,768]{1,0:T(8,128)(2,1)}, bf16[32,768]{1,0:T(8,128)(2,1)}) async-done(((bf16[32,768]{1,0:T(8,128)(2,1)}, bf16[32,768]{1,0:T(8,128)(2,1)}), (bf16[32,768]{1,0:T(8,128)(2,1)}, bf16[32,768]{1,0:T(8,128)(2,1)})) %all-reduce.3.cloned.1.call-update) | async-done | bytes 98320 | tf_op jit(solution)/shard_map/psum | solution.py:13
  87.8 0.8 convert_multiply_fusion.1
  88.6 17.2 %divide_convert_fusion.1 = bf16[32,256,768]{2,1,0:T(8,128)(2,1)} fusion(f32[32,256,768]{2,1,0:T(8,128)} %param.6, bf16[32,256,768]{2,1,0:T(8,128)(2,1)} %param.7, f32[32,768]{1,0:T(8,128)S(1)} %convert_multiply_fusion.1), kind=kLoop, calls=%fused_computation.3 | loop fusion | flops 25165824 | bytes 50429952 | tf_op jit(solution)/shard_map/convert_element_type | solution.py:23
  105.9 0.0 copy-start
  105.9 5.5 all-to-all-start
  111.3 0.0 copy-done
  111.4 17.4 %divide_convert_fusion = bf16[32,256,768]{2,1,0:T(8,128)(2,1)} fusion(f32[32,256,768]{2,1,0:T(8,128)} %param.8, bf16[32,256,768]{2,1,0:T(8,128)(2,1)} %param.9, f32[32,768]{1,0:T(8,128)S(1)} %convert_multiply_fusion), kind=kLoop, calls=%fused_computation | loop fusion | flops 25165824 | bytes 50429952 | tf_op jit(solution)/shard_map/convert_element_type | solution.py:24
  128.7 0.0 copy-start.1
  128.7 0.0 copy-start.2
  128.7 256.4 %all-to-all-done = bf16[32,256,768]{2,1,0:T(8,128)(2,1)} async-done(((bf16[32,256,768]{2,1,0:T(8,128)(2,1)}), bf16[32,256,768]{2,1,0:T(8,128)(2,1)}, u32[]{:S(2)}, u32[]{:S(2)}) %all-to-all-start) | async-done | bytes 12582944 | tf_op jit(solution)/shard_map/all_to_all | solution.py:27
  385.1 5.4 all-to-all-start.1
  390.5 0.0 copy-done.1
  390.5 0.0 copy-done.2
  390.6 280.0 %all_gather.6 = bf16[2048,32]{0,1:T(8,128)(2,1)S(1)} all-gather(bf16[256,32]{0,1:T(8,128)(2,1)S(1)} %multiply_convert_fusion), channel_id=1, replica_groups=mesh['ep'=4,'fsdp'=8] {'fsdp'}, dimensions={0}, use_global_device_ids=true | all-gather | bytes 147456 | tf_op jit(solution)/shard_map/all_gather | solution.py:37
  670.5 10.3 %all_gather.7 = bf16[2048,128]{0,1:T(8,128)(2,1)S(1)} all-gather(bf16[2048,32]{0,1:T(8,128)(2,1)S(1)} %all_gather.6), channel_id=1, replica_groups=mesh['ep'=4,'fsdp'=8] {'ep'}, dimensions={1}, use_global_device_ids=true | all-gather | bytes 655360 | tf_op jit(solution)/shard_map/all_gather | solution.py:38
  680.8 1.0 copy.16
  681.8 0.6 constant_dynamic-slice_fusion
  682.4 0.6 constant_dynamic-slice_fusion.1
  683.0 10.7 %copy.14 = bf16[8,4,256,768]{3,2,0,1:T(8,128)(2,1)} copy(bf16[8,4,256,768]{3,2,1,0:T(8,128)(2,1)} %bitcast) | data formatting | bytes 25165824 | tf_op jit(solution)/shard_map/all_to_all | solution.py:27
  693.7 0.0 all-to-all-done.1
  693.7 10.7 %copy.15 = bf16[8,4,256,768]{3,2,0,1:T(8,128)(2,1)} copy(bf16[8,4,256,768]{3,2,1,0:T(8,128)(2,1)} %bitcast.3) | data formatting | bytes 25165824 | tf_op jit(solution)/shard_map/all_to_all | solution.py:28
  (2 shorter events, 0.0 us)
Async XLA Ops:
  7.2 80.6 %all-reduce.3.cloned.1.call-start = ((), (), s32[]{:S(2)}) async-start(), calls=%async_computation.2 | async-start | bytes 196608 | tf_op jit(solution)/shard_map/psum | solution.py:13
  105.9 5.5 copy-start
  105.9 279.3 %all-to-all-start = ((bf16[32,256,768]{2,1,0:T(8,128)(2,1)}), bf16[32,256,768]{2,1,0:T(8,128)(2,1)}, u32[]{:S(2)}, u32[]{:S(2)}) async-start(bf16[32,256,768]{2,1,0:T(8,128)(2,1)} %divide_convert_fusion.1), calls=%async_computation | async-start | bytes 25165824 | tf_op jit(solution)/shard_map/all_to_all | solution.py:27
  128.7 261.8 %copy-start.1 = (f32[256,32]{0,1:T(8,128)S(1)}, f32[256,32]{0,1:T(8,128)}, u32[]{:S(2)}) copy-start(f32[256,32]{0,1:T(8,128)} %param.10) | copy-start | bytes 98308
  128.7 261.8 %copy-start.2 = (f32[256]{0:T(256)S(1)}, f32[256]{0:T(256)}, u32[]{:S(2)}) copy-start(f32[256]{0:T(256)} %param.11) | copy-start | bytes 3076
  385.1 308.5 %all-to-all-start.1 = ((bf16[32,256,768]{2,1,0:T(8,128)(2,1)}), bf16[32,256,768]{2,1,0:T(8,128)(2,1)}, u32[]{:S(2)}, u32[]{:S(2)}) async-start(bf16[32,256,768]{2,1,0:T(8,128)(2,1)} %divide_convert_fusion), calls=%async_computation.1 | async-start | bytes 25165824 | tf_op jit(solution)/shard_map/all_to_all | solution.py:28
Sparse Core Ops, SparseCore 0:
  32.5 55.2 all-reduce.2
where the time goes:
time: 712 us; the launch traced here: 711 us
  waiting for transfers between devices  312 us (44%)
  blocking collectives  290 us (41%)
  other arithmetic  60.6 us (9%)
  local copies, waits for them, and re-layouts  23.6 us (3%)
  between operations  14.1 us (2%)
  starting transfers between devices  10.9 us (2%)
    all_gather x1, blocking collectives, shards(): row_router = lax.all_gather(part_router, 'fsdp', axis=0, tiled=True)  280 us
    all_to_all x1, waiting for transfers between devices, shards(): lax.all_to_all(narrow_gate, 'fsdp', split_axis=0, concat_axis=1, tiled=True)  256 us
    psum x1, waiting for transfers between devices, shards(): lax.psum(jnp.sum(jnp.abs(latest_gate), axis=1).astype(jnp.bfloat16), 'fsdp')  55.4 us
    reduce_sum x1, other arithmetic, shards(): jnp.sum(jnp.abs(latest_up), axis=1).astype(jnp.bfloat16)  25.2 us
    convert_element_type x1, other arithmetic, shards(): (latest_up / jnp.expand_dims(scale_up, 1)).astype(jnp.bfloat16)  17.4 us
    convert_element_type x1, other arithmetic, shards(): (latest_gate / jnp.expand_dims(scale_gate, 1)).astype(jnp.bfloat16)  17.2 us
  transfers between devices with their start and end apart: 3, of which 2 were waited for; matrix products, arithmetic and copies ran while one was open for 4% of the time, Pallas kernels for 0%

commit v1 on v0

--- a/solution.py
+++ b/solution.py
@@ -2,6 +2,7 @@
 import jax.numpy as jnp
 from jax import lax
 from jax.sharding import PartitionSpec as P
+from jax.lax import all_gather
 
 D_MODEL = 2048
 
@@ -9,8 +10,13 @@
 def shards(train_gate, other_gate, train_up, other_up, router_weight, router_gain):
     latest_gate = train_gate + other_gate.astype(jnp.float32)
     latest_up = train_up + other_up.astype(jnp.float32)
+
+    def register_the_roads(inp):
+        side_arr = all_gather(inp, "fsdp").sum(axis=0)
+        return side_arr
+
     total_gate, total_up = (
-        lax.psum(jnp.sum(jnp.abs(latest_gate), axis=1).astype(jnp.bfloat16), "fsdp").astype(
+        register_the_roads(jnp.sum(jnp.abs(latest_gate), axis=1).astype(jnp.bfloat16)).astype(
             jnp.float32
         ),
         lax.psum(jnp.sum(jnp.abs(latest_up), axis=1).astype(jnp.bfloat16), "fsdp").astype(

time: 712 us -> 679 us (0.954)
  waiting for transfers between devices: 312 us -> 0.01 us
  blocking collectives: 290 us -> 582 us
  between operations: 14.1 us -> 0.72 us
    psum x0 -> x1, blocking collectives: none -> 276 us  [shards(): lax.psum(jnp.sum(jnp.abs(latest_up), axis=1).astype(jnp.bfloat16), 'fsdp')]
    all_to_all x1, waiting for transfers between devices: 256 us -> 0.01 us  [shards(): lax.all_to_all(narrow_gate, 'fsdp', split_axis=0, concat_axis=1, tiled=True)]
    psum x1 -> x0, waiting for transfers between devices: 55.4 us -> none  [shards(): lax.psum(jnp.sum(jnp.abs(latest_gate), axis=1).astype(jnp.bfloat16), 'fsdp')]
    all_gather x0 -> x1, blocking collectives: none -> 16.2 us  [register_the_roads(): side_arr = all_gather(inp, 'fsdp').sum(axis=0)]
    reduce_sum x0 -> x2, other arithmetic: none -> 12.9 us  [the longest x1 12.8 us: shards(): jnp.sum(jnp.abs(latest_gate), axis=1).astype(jnp.bfloat16)]
    reduce_sum x1, other arithmetic: 25.2 us -> 12.8 us  [shards(): jnp.sum(jnp.abs(latest_up), axis=1).astype(jnp.bfloat16)]
  transfers between devices with their start and end apart: 3 -> 2, of which waited for: 2 -> 0; matrix products, arithmetic and copies ran while one was open for 4% -> 6% of each run, Pallas kernels for 0% -> 0%
where the time goes in v1:
time: 679 us; the launch traced here: 678 us
  blocking collectives  582 us (86%)
  other arithmetic  60.4 us (9%)
  local copies, waits for them, and re-layouts  23.6 us (3%)
  starting transfers between devices  10.9 us (2%)
    all_gather x1, blocking collectives, shards(): row_router = lax.all_gather(part_router, 'fsdp', axis=0, tiled=True)  280 us
    psum x1, blocking collectives, shards(): lax.psum(jnp.sum(jnp.abs(latest_up), axis=1).astype(jnp.bfloat16), 'fsdp')  276 us
    convert_element_type x1, other arithmetic, shards(): (latest_up / jnp.expand_dims(scale_up, 1)).astype(jnp.bfloat16)  17.4 us
    convert_element_type x1, other arithmetic, shards(): (latest_gate / jnp.expand_dims(scale_gate, 1)).astype(jnp.bfloat16)  17.2 us
    all_gather x1, blocking collectives, register_the_roads(): side_arr = all_gather(inp, 'fsdp').sum(axis=0)  16.2 us
  transfers between devices with their start and end apart: 2, of which 0 were waited for; matrix products, arithmetic and copies ran while one was open for 6% of the time, Pallas kernels for 0%

profile of v1, /device:TPU:0, one launch (start us, length us, event | category | flops | bytes accessed | tf_op | source)
XLA Modules:
  0.0 678.1 jit_solution(15375657672300780454)
XLA Ops:
  0.6 12.8 %abs_reduce_fusion.1 = bf16[32,768]{1,0:T(8,128)(2,1)S(1)} fusion(f32[32,256,768]{2,1,0:T(8,128)} %param.6, bf16[32,256,768]{2,1,0:T(8,128)(2,1)} %param.7), kind=kLoop, calls=%fused_computation.4 | loop fusion | flops 25141248 | bytes 37797888 | tf_op jit(solution)/shard_map/reduce_sum | solution.py:19
  13.5 16.2 %all-gather = bf16[256,768]{1,0:T(8,128)(2,1)S(1)} all-gather(bf16[32,768]{1,0:T(8,128)(2,1)S(1)} %abs_reduce_fusion.1), channel_id=2, replica_groups=mesh['ep'=4,'fsdp'=8] {'fsdp'}, dimensions={0}, use_global_device_ids=true | all-gather | bytes 442368 | tf_op jit(solution)/shard_map/all_gather | solution.py:15
  29.7 0.1 reduce_sum.31
  29.8 17.2 %divide_convert_fusion.1 = bf16[32,256,768]{2,1,0:T(8,128)(2,1)} fusion(f32[32,256,768]{2,1,0:T(8,128)} %param.6, bf16[32,256,768]{2,1,0:T(8,128)(2,1)} %param.7, f32[32,768]{1,0:T(8,128)S(1)} %convert_multiply_fusion.1), kind=kLoop, calls=%fused_computation.3 | loop fusion | flops 25165824 | bytes 50429952 | tf_op jit(solution)/shard_map/convert_element_type | solution.py:29
  47.0 5.3 all-to-all-start
  52.4 12.8 %abs_reduce_fusion = bf16[32,768]{1,0:T(8,128)(2,1)S(1)} fusion(f32[32,256,768]{2,1,0:T(8,128)} %param.8, bf16[32,256,768]{2,1,0:T(8,128)(2,1)} %param.9), kind=kLoop, calls=%fused_computation.1 | loop fusion | flops 25141248 | bytes 37797888 | tf_op jit(solution)/shard_map/reduce_sum | solution.py:22
  65.2 276.0 %psum.7 = bf16[32,768]{1,0:T(8,128)(2,1)S(1)} all-reduce(bf16[32,768]{1,0:T(8,128)(2,1)S(1)} %abs_reduce_fusion), channel_id=1, replica_groups=mesh['ep'=4,'fsdp'=8] {'fsdp'}, use_global_device_ids=true, to_apply=%region_3.0 | all-reduce | flops 24576 | bytes 98304 | tf_op jit(solution)/shard_map/psum | solution.py:22
  341.2 17.4 %divide_convert_fusion = bf16[32,256,768]{2,1,0:T(8,128)(2,1)} fusion(f32[32,256,768]{2,1,0:T(8,128)} %param.8, bf16[32,256,768]{2,1,0:T(8,128)(2,1)} %param.9, f32[32,768]{1,0:T(8,128)S(1)} %convert_multiply_fusion), kind=kLoop, calls=%fused_computation | loop fusion | flops 25165824 | bytes 50429952 | tf_op jit(solution)/shard_map/convert_element_type | solution.py:30
  358.6 0.0 copy-start
  358.6 0.0 copy-start.1
  358.6 0.0 all-to-all-done
  358.7 5.5 all-to-all-start.1
  364.2 0.0 copy-done
  364.2 0.0 copy-done.1
  364.2 280.0 %all_gather.11 = bf16[2048,32]{0,1:T(8,128)(2,1)S(1)} all-gather(bf16[256,32]{0,1:T(8,128)(2,1)S(1)} %multiply_convert_fusion), channel_id=1, replica_groups=mesh['ep'=4,'fsdp'=8] {'fsdp'}, dimensions={0}, use_global_device_ids=true | all-gather | bytes 147456 | tf_op jit(solution)/shard_map/all_gather | solution.py:43
  644.2 10.3 %all_gather.12 = bf16[2048,128]{0,1:T(8,128)(2,1)S(1)} all-gather(bf16[2048,32]{0,1:T(8,128)(2,1)S(1)} %all_gather.11), channel_id=1, replica_groups=mesh['ep'=4,'fsdp'=8] {'ep'}, dimensions={1}, use_global_device_ids=true | all-gather | bytes 655360 | tf_op jit(solution)/shard_map/all_gather | solution.py:44
  654.5 1.0 copy.19
  655.5 0.6 constant_dynamic-slice_fusion.1
  656.1 0.6 constant_dynamic-slice_fusion
  656.7 10.7 %copy.17 = bf16[8,4,256,768]{3,2,0,1:T(8,128)(2,1)} copy(bf16[8,4,256,768]{3,2,1,0:T(8,128)(2,1)} %bitcast.1) | data formatting | bytes 25165824 | tf_op jit(solution)/shard_map/all_to_all | solution.py:33
  667.4 0.0 all-to-all-done.1
  667.4 10.7 %copy.18 = bf16[8,4,256,768]{3,2,0,1:T(8,128)(2,1)} copy(bf16[8,4,256,768]{3,2,1,0:T(8,128)(2,1)} %bitcast.4) | data formatting | bytes 25165824 | tf_op jit(solution)/shard_map/all_to_all | solution.py:34
  (3 shorter events, 0.0 us)
Async XLA Ops:
  47.0 311.6 %all-to-all-start = ((bf16[32,256,768]{2,1,0:T(8,128)(2,1)}), bf16[32,256,768]{2,1,0:T(8,128)(2,1)}, u32[]{:S(2)}, u32[]{:S(2)}) async-start(bf16[32,256,768]{2,1,0:T(8,128)(2,1)} %divide_convert_fusion.1), calls=%async_computation | async-start | bytes 25165824 | tf_op jit(solution)/shard_map/all_to_all | solution.py:33
  358.6 5.6 copy-start
  358.6 5.6 copy-start.1
  358.7 308.7 %all-to-all-start.1 = ((bf16[32,256,768]{2,1,0:T(8,128)(2,1)}), bf16[32,256,768]{2,1,0:T(8,128)(2,1)}, u32[]{:S(2)}, u32[]{:S(2)}) async-start(bf16[32,256,768]{2,1,0:T(8,128)(2,1)} %divide_convert_fusion), calls=%async_computation.1 | async-start | bytes 25165824 | tf_op jit(solution)/shard_map/all_to_all | solution.py:34
